TPU v7x, 256 devices: a whole 4x4x8 slice. The times are simulated.
256 devices in a mesh: expert: 32 (over z_hi, y, core), dp: 8 (over z_lo, x).
Axes of the slice: x: 4, y: 4, z: 8 (z_hi: 4, z_lo: 2; z = z_hi * 2 + z_lo), core: 2. Of those that a mesh axis runs over, the one named last changes fastest.
Arguments:
- tokens: bfloat16 [32768, 4096], P(('expert', 'dp')), may hold values from -6 to 6
- route: int32 [32768, 2], P(('expert', 'dp')), may hold values from 0 to 63, all different within a row; in each aligned block of 128 rows (0 to 127, 128 to 255, ...) at most 12 rows name the same one
- gate_output_gradient: bfloat16 [32768, 2, 1536], P(('expert', 'dp')), may hold values from -0.4375 to 0.4375
- frozen_gate_weight: bfloat16 [64, 4096, 1536], P('expert', 'dp'), may hold values from -0.09375 to 0.09375
- adapter_first: bfloat16 [64, 4096, 16], P('expert'), may hold values from -0.09375 to 0.09375
- adapter_second: bfloat16 [64, 16, 1536], P('expert'), may hold values from -0.15625 to 0.15625
Outputs:
- grad_a: float32 [64, 4096, 16], P('expert')
- grad_b: float32 [64, 16, 1536], P('expert')
Inputs may be any that keep to these rules, and one draw needn't show every extreme that they name: `route`: each row names 2 different experts. Within each device's aligned block of 128 rows no expert is named more than 12 times.
All inputs are finite; a program needn't handle non-finite values.
Results may differ from a plain program's by a relative error of at most 0.0043.
Values may be sent and summed in bfloat16 or wider, within the bound.
No kernel may reach another device: no remote copies, remote signals or barrier semaphores. Data moves between devices by JAX's collectives and lax.ppermute only.
A program may use at most 128 MiB of HBM per device.

v0:
```python
import jax
import jax.numpy as jnp
from jax import lax
from jax.sharding import PartitionSpec as P

ADAPTER_SCALE = 2.0


def silu_slope(gate_preactivation):
    squash = jax.nn.sigmoid(gate_preactivation)
    return squash * (1.0 + gate_preactivation * (1.0 - squash))


def block_product(input_rows, piece):
    return jnp.dot(input_rows, piece, preferred_element_type=jnp.float32)


def prepare(input_rows, rows_g):
    block = 128
    return (input_rows, rows_g, None, block)


def adapter_grads(input_rows, rows_g, frozen_output, first_adapter_factor, second_adapter_factor):
    rank_reduced_output = jnp.dot(
        input_rows, first_adapter_factor, preferred_element_type=jnp.float32
    ).astype(jnp.bfloat16)
    gate_preactivation = frozen_output + ADAPTER_SCALE * jnp.dot(
        rank_reduced_output, second_adapter_factor, preferred_element_type=jnp.float32
    )
    activation_slope = (rows_g.astype(jnp.float32) * silu_slope(gate_preactivation)).astype(
        jnp.bfloat16
    )
    up_gradient = ADAPTER_SCALE * jnp.einsum(
        "nr,nf->rf", rank_reduced_output, activation_slope, preferred_element_type=jnp.float32
    )
    rank_backward = jnp.einsum(
        "nf,rf->nr", activation_slope, second_adapter_factor, preferred_element_type=jnp.float32
    ).astype(jnp.bfloat16)
    down_gradient = ADAPTER_SCALE * jnp.einsum(
        "nd,nr->dr", input_rows, rank_backward, preferred_element_type=jnp.float32
    )
    return (down_gradient, up_gradient)


def local(tokens, route, gate_output_gradient, frozen_gate_weight, adapter_first, adapter_second):
    experts_here = frozen_gate_weight.shape[0]
    columns = lax.axis_size("expert")
    experts = experts_here * columns
    tok_rows = tokens.shape[0]
    top_count = route.shape[1]
    width = tokens.shape[1]
    hidden = gate_output_gradient.shape[2]
    capacity = 3 * tok_rows * top_count // experts
    slot_count = tok_rows * top_count
    flat_route = route.reshape(slot_count)
    labels = jnp.arange(experts, dtype=jnp.int32)
    one_hot = (flat_route[:, None] == labels[None, :]).astype(jnp.int32)
    ranks = jnp.sum((jnp.cumsum(one_hot, axis=0) - one_hot) * one_hot, axis=1)
    target = (flat_route % experts_here * columns + flat_route // experts_here) * capacity + ranks
    positions = jnp.arange(experts * capacity, dtype=jnp.int32)
    hits = target[None, :] == positions[:, None]
    filled = jnp.any(hits, axis=1)
    slot_ids = jnp.arange(slot_count, dtype=jnp.int32)
    source_slot = jnp.sum(jnp.where(hits, slot_ids[None, :], 0), axis=1)
    send_x = tokens[source_slot // top_count].reshape(experts_here, columns, capacity, width)
    flat_grad = gate_output_gradient.reshape(slot_count, hidden)
    send_g = jnp.where(
        filled[:, None], flat_grad[source_slot], jnp.zeros((), gate_output_gradient.dtype)
    )
    send_g = send_g.reshape(experts_here, columns, capacity, hidden)
    group_rows = columns * capacity
    recv_x, recv_g = (
        lax.all_to_all(send_x, "expert", split_axis=1, concat_axis=1, tiled=True),
        lax.all_to_all(send_g, "expert", split_axis=1, concat_axis=1, tiled=True),
    )
    input_rows = recv_x.reshape(experts_here, group_rows, width)
    rows_g = recv_g.reshape(experts_here, group_rows, hidden)
    ready_inputs = [
        prepare(input_rows[local_result], rows_g[local_result])
        for local_result in range(experts_here)
    ]

    def add_rows(piece):
        return jnp.stack(
            [
                block_product(ready_inputs[local_result][0], piece[local_result])
                for local_result in range(experts_here)
            ]
        )

    frozen_output = add_rows(lax.all_gather(frozen_gate_weight, "dp", axis=1, tiled=True))
    results = [
        adapter_grads(
            ready_inputs[local_result][0],
            ready_inputs[local_result][1],
            frozen_output[local_result],
            adapter_first[local_result],
            adapter_second[local_result],
        )
        for local_result in range(experts_here)
    ]
    grad_a_local = jnp.stack([result[0] for result in results])
    grad_b_local = jnp.stack([result[1] for result in results])
    grad_a, grad_b = lax.psum((grad_a_local, grad_b_local), "dp")
    return (grad_a, grad_b)


def solution(mesh):
    return jax.shard_map(
        local,
        mesh=mesh,
        in_specs=(
            P(("expert", "dp"), None),
            P(("expert", "dp"), None),
            P(("expert", "dp"), None, None),
            P("expert", "dp", None),
            P("expert", None, None),
            P("expert", None, None),
        ),
        out_specs=(P("expert", None, None), P("expert", None, None)),
        check_vma=False,
    )
```

profile of v0, /device:TPU:8, one launch (start us, length us, event | category | flops | bytes accessed | tf_op | source)
XLA Modules:
  0.0 568.3 jit_solution(11198235258273988007)
XLA Ops:
  7.2 0.0 all-gather.2.cloned.1.call-start
  7.2 0.7 all-gather.2.cloned.1.call-update
  7.9 0.0 copy-done.8
  7.9 0.1 copy.16
  8.1 0.1 eq.41
  8.2 0.1 reshape.174
  8.4 0.6 reduce-window.6
  9.0 0.2 slice_reduce_fusion.2
  9.2 0.3 reshape.177
  9.5 0.1 fusion.17
  9.6 0.2 select_reduce_fusion
  9.9 3.9 gather_fusion.1
  13.7 4.8 gather.10
  18.5 0.2 fusion.10
  18.7 0.1 broadcast_in_dim.35
  18.8 2.2 broadcast_select_fusion
  21.0 3.8 copy.20
  24.8 11.7 %all-to-all-start.1 = ((bf16[2,32,12,1536]{3,0,2,1:T(2,128)(2,1)}), bf16[2,32,12,1536]{3,0,2,1:T(2,128)(2,1)S(1)}, u32[]{:S(2)}, u32[]{:S(2)}) async-start(bf16[2,32,12,1536]{3,0,2,1:T(2,128)(2,1)} %copy.20), calls=%async_computation.1 | async-start | bytes 4718592 | tf_op jit(solution)/shard_map/all_to_all | solution.py:74
  36.6 5.7 gather_fusion
  42.2 9.8 %reshape.176 = bf16[2,32,12,4096]{3,2,1,0:T(8,128)(2,1)} reshape(bf16[768,4096]{1,0:T(8,128)(2,1)} %gather_fusion) | data formatting | bytes 12582912 | tf_op jit(solution)/shard_map/reshape | solution.py:65
  52.0 13.6 %copy.19 = bf16[2,32,12,4096]{3,0,2,1:T(2,128)(2,1)} copy(bf16[2,32,12,4096]{3,2,1,0:T(8,128)(2,1)} %reshape.176) | data formatting | bytes 12582912 | tf_op jit(solution)/shard_map/reshape | solution.py:65
  65.5 53.0 %all-to-all-done.1 = bf16[2,32,12,1536]{3,0,2,1:T(2,128)(2,1)S(1)} async-done(((bf16[2,32,12,1536]{3,0,2,1:T(2,128)(2,1)}), bf16[2,32,12,1536]{3,0,2,1:T(2,128)(2,1)S(1)}, u32[]{:S(2)}, u32[]{:S(2)}) %all-to-all-start.1) | async-done | bytes 2359328 | tf_op jit(solution)/shard_map/all_to_all | solution.py:74
  118.6 5.3 all-to-all-start
  123.9 0.0 all-reduce.3.cloned.1.call-start
  124.0 15.2 %fusion.7 = (f32[32,12,1536]{2,1,0:T(8,128)}, f32[32,12,1536]{2,1,0:T(8,128)}) fusion(bf16[2,32,12,1536]{3,0,2,1:T(2,128)(2,1)S(1)} %all-to-all-done.1), kind=kLoop, calls=%fused_computation.20 | loop fusion | flops 1179648 | bytes 7077888 | tf_op jit(solution)/shard_map/convert_element_type | solution.py:30
  139.1 3.6 reshape.178
  142.7 3.6 reshape.179
  146.2 186.4 %all-to-all-done = bf16[2,32,12,4096]{3,0,2,1:T(2,128)(2,1)} async-done(((bf16[2,32,12,4096]{3,0,2,1:T(2,128)(2,1)}), bf16[2,32,12,4096]{3,0,2,1:T(2,128)(2,1)}, u32[]{:S(2)}, u32[]{:S(2)}) %all-to-all-start) | async-done | bytes 6291488 | tf_op jit(solution)/shard_map/all_to_all | solution.py:73
  332.6 33.0 %slice_reduce_fusion.1 = (bf16[32,12,4096]{2,1,0:T(8,128)(2,1)}, bf16[32,12,4096]{2,1,0:T(8,128)(2,1)}) fusion(bf16[2,32,12,4096]{3,0,2,1:T(2,128)(2,1)} %all-to-all-done), kind=kLoop, calls=%fused_computation.7 | loop fusion | bytes 12582912 | tf_op jit(solution)/shard_map/slice | solution.py:79
  365.6 5.6 squeeze.26
  371.2 5.6 squeeze.30
  376.8 3.0 convolution_convert_fusion.3
  379.8 0.9 convolution_convert_fusion.1
  380.8 69.1 %all-gather.2.cloned.1.call-done = bf16[2,4096,1536]{2,1,0:T(8,128)(2,1)} async-done(((bf16[2,512,1536]{2,1,0:T(8,128)(2,1)}), bf16[2,4096,1536]{2,1,0:T(8,128)(2,1)}) %all-gather.2.cloned.1.call-update) | async-done | bytes 25165840 | tf_op jit(solution)/shard_map/all_gather | solution.py:91
  449.8 9.3 %fusion.1 = f32[384,1536]{1,0:T(8,128)S(1)} fusion(bf16[384,4096]{1,0:T(8,128)(2,1)} %squeeze.26, bf16[2,4096,1536]{2,1,0:T(8,128)(2,1)} %all-gather.2.cloned.1.call-done), kind=kOutput, calls=%fused_computation.5 | convolution fusion | flops 4831838208 | bytes 18087936 | tf_op jit(solution)/shard_map/dot_general | solution.py:15
  459.2 1.1 multiply_convert_fusion.1
  460.3 0.3 fusion.8
  460.6 3.0 fusion.3
  463.6 9.1 %fusion = f32[384,1536]{1,0:T(8,128)S(1)} fusion(bf16[384,4096]{1,0:T(8,128)(2,1)} %squeeze.30, bf16[2,4096,1536]{2,1,0:T(8,128)(2,1)} %all-gather.2.cloned.1.call-done), kind=kOutput, calls=%fused_computation.3 | convolution fusion | flops 4831838208 | bytes 18087936 | tf_op jit(solution)/shard_map/dot_general | solution.py:15
  472.7 1.1 multiply_convert_fusion
  473.8 0.3 fusion.9
  474.1 3.1 fusion.2
  477.2 0.7 pad_maximum_fusion.1
  477.9 0.8 pad_maximum_fusion
  478.7 0.0 all-reduce.3.cloned.1.call-update
  478.7 79.3 %all-reduce.3.cloned.1.call-done = (f32[2,4096,16]{1,2,0:T(8,128)}, f32[2,16,1536]{2,1,0:T(8,128)}) async-done(((f32[2,4096,16]{1,2,0:T(8,128)}, f32[2,16,1536]{2,1,0:T(8,128)}), (f32[2,4096,16]{1,2,0:T(8,128)}, f32[2,16,1536]{2,1,0:T(8,128)})) %all-reduce.3.cloned.1.call-update) | async-done | bytes 720912 | tf_op jit(solution)/shard_map/psum | solution.py:104
  558.0 1.9 copy.29
  559.9 1.6 copy.30
  (23 shorter events, 0.2 us)
Async XLA Ops:
  7.2 29.4 %copy-start = (bf16[128,4096]{1,0:T(8,128)(2,1)S(1)}, bf16[128,4096]{1,0:T(8,128)(2,1)}, u32[]{:S(2)}) copy-start(bf16[128,4096]{1,0:T(8,128)(2,1)} %param.6) | copy-start | bytes 3145732
  7.2 0.8 copy-start.8
  7.2 2.0 copy-start.5
  7.2 442.6 %all-gather.2.cloned.1.call-start = ((), (), s32[]{:S(2)}) async-start(), calls=%async_computation.2 | async-start | bytes 28311552 | tf_op jit(solution)/shard_map/all_gather | solution.py:91
  24.8 93.7 %all-to-all-start.1 = ((bf16[2,32,12,1536]{3,0,2,1:T(2,128)(2,1)}), bf16[2,32,12,1536]{3,0,2,1:T(2,128)(2,1)S(1)}, u32[]{:S(2)}, u32[]{:S(2)}) async-start(bf16[2,32,12,1536]{3,0,2,1:T(2,128)(2,1)} %copy.20), calls=%async_computation.1 | async-start | bytes 4718592 | tf_op jit(solution)/shard_map/all_to_all | solution.py:74
  118.6 214.0 %all-to-all-start = ((bf16[2,32,12,4096]{3,0,2,1:T(2,128)(2,1)}), bf16[2,32,12,4096]{3,0,2,1:T(2,128)(2,1)}, u32[]{:S(2)}, u32[]{:S(2)}) async-start(bf16[2,32,12,4096]{3,0,2,1:T(2,128)(2,1)} %copy.19), calls=%async_computation | async-start | bytes 12582912 | tf_op jit(solution)/shard_map/all_to_all | solution.py:73
  123.9 434.1 %all-reduce.3.cloned.1.call-start = ((), (), s32[]{:S(2)}) async-start(), calls=%async_computation.3 | async-start | bytes 1441792 | tf_op jit(solution)/shard_map/psum | solution.py:104
  371.2 5.6 copy-start.6
  376.8 3.0 copy-start.2
  380.8 78.4 %copy-start.7 = (bf16[2,16,1536]{2,1,0:T(8,128)(2,1)S(1)}, bf16[2,16,1536]{2,1,0:T(8,128)(2,1)}, u32[]{:S(2)}) copy-start(bf16[2,16,1536]{2,1,0:T(8,128)(2,1)} %param.11) | copy-start | bytes 294916
  449.8 9.3 %copy-start.4 = (f32[384,1536]{1,0:T(8,128)S(1)}, f32[384,1536]{1,0:T(8,128)}, u32[]{:S(2)}) copy-start(f32[384,1536]{1,0:T(8,128)} %reshape.178) | copy-start | bytes 7077892
  463.6 9.1 %copy-start.3 = (f32[384,1536]{1,0:T(8,128)S(1)}, f32[384,1536]{1,0:T(8,128)}, u32[]{:S(2)}) copy-start(f32[384,1536]{1,0:T(8,128)} %reshape.179) | copy-start | bytes 7077892
  474.1 87.4 %copy-start.1 = (bf16[128,4096]{1,0:T(8,128)(2,1)S(1)}, bf16[128,4096]{1,0:T(8,128)(2,1)}, u32[]{:S(2)}) copy-start(bf16[128,4096]{1,0:T(8,128)(2,1)} %param.6) | copy-start | bytes 3145732
Sparse Core Ops, SparseCore 0:
  9.8 439.9 all-gather.1
  478.8 79.1 all-reduce.2
where the time goes:
time: 569 us; the launch traced here: 568 us
  waiting for transfers between devices  388 us (68%)
  local copies, waits for them, and re-layouts  97.3 us (17%)
  matrix products  31.2 us (5%)
  other arithmetic  20 us (4%)
  starting transfers between devices  17.1 us (3%)
  between operations  14.2 us (2%)
    all_to_all x1, waiting for transfers between devices, local(): lax.all_to_all(send_x, 'expert', split_axis=1, concat_axis=1, tiled=True)  186 us
    psum x1, waiting for transfers between devices, local(): grad_a, grad_b = lax.psum((grad_a_local, grad_b_local), 'dp')  79.3 us
    all_gather x1, waiting for transfers between devices, local(): lax.all_gather(frozen_gate_weight, 'dp', axis=1, tiled=True)  69.1 us
    all_to_all x1, waiting for transfers between devices, local(): lax.all_to_all(send_g, 'expert', split_axis=1, concat_axis=1, tiled=True)  53 us
    slice x1, local copies, waits for them, and re-layouts, local(): input_rows[local_result]  33 us
    reshape x2, local copies, waits for them, and re-layouts, local(): tokens[source_slot // top_count]  23.3 us
    dot_general x2, matrix products, block_product(): return jnp.dot(input_rows, piece, preferred_element_type=jnp.float32)  18.4 us
    convert_element_type x1, other arithmetic, adapter_grads(): rows_g.astype(jnp.float32) * silu_slope(gate_preactivation)  15.2 us
  transfers between devices with their start and end apart: 4, of which 4 were waited for; matrix products, arithmetic and copies ran while one was open for 20% of the time, Pallas kernels for 0%

commit v1 on v0

--- a/solution.py
+++ b/solution.py
@@ -4,6 +4,12 @@
 from jax.sharding import PartitionSpec as P
 
 ADAPTER_SCALE = 2.0
+
+
+def gather_blocks(x, axis, dim):
+    parts = lax.all_gather(x, axis, axis=0, tiled=False)
+    full = jnp.concatenate(parts, axis=dim)
+    return full
 
 
 def silu_slope(gate_preactivation):
@@ -88,7 +94,7 @@
             ]
         )
 
-    frozen_output = add_rows(lax.all_gather(frozen_gate_weight, "dp", axis=1, tiled=True))
+    frozen_output = add_rows(gather_blocks(frozen_gate_weight, "dp", 1))
     results = [
         adapter_grads(
             ready_inputs[local_result][0],

time: 569 us -> 579 us (1.018)
  local copies, waits for them, and re-layouts: 97.3 us -> 111 us
    slice x1 -> x2, local copies, waits for them, and re-layouts: 0.18 us -> 14 us  [the longest x1 13.8 us: add_rows(): piece[local_result]]
where the time goes in v1:
time: 579 us; the launch traced here: 578 us
  waiting for transfers between devices  388 us (67%)
  local copies, waits for them, and re-layouts  111 us (19%)
  matrix products  27 us (5%)
  other arithmetic  19.9 us (3%)
  starting transfers between devices  17.3 us (3%)
  between operations  14.2 us (2%)
    all_to_all x1, waiting for transfers between devices, local(): lax.all_to_all(send_x, 'expert', split_axis=1, concat_axis=1, tiled=True)  186 us
    psum x1, waiting for transfers between devices, local(): grad_a, grad_b = lax.psum((grad_a_local, grad_b_local), 'dp')  79.3 us
    all_gather x1, waiting for transfers between devices, gather_blocks(): parts = lax.all_gather(x, axis, axis=0, tiled=False)  69 us
    all_to_all x1, waiting for transfers between devices, local(): lax.all_to_all(send_g, 'expert', split_axis=1, concat_axis=1, tiled=True)  53 us
    slice x1, local copies, waits for them, and re-layouts, local(): input_rows[local_result]  33 us
    reshape x2, local copies, waits for them, and re-layouts, local(): tokens[source_slot // top_count]  23.3 us
    convert_element_type x1, other arithmetic, adapter_grads(): rows_g.astype(jnp.float32) * silu_slope(gate_preactivation)  15 us
    dot_general x2, matrix products, block_product(): return jnp.dot(input_rows, piece, preferred_element_type=jnp.float32)  14.2 us
  transfers between devices with their start and end apart: 4, of which 4 were waited for; matrix products, arithmetic and copies ran while one was open for 20% of the time, Pallas kernels for 0%

profile of v1, /device:TPU:8, one launch (start us, length us, event | category | flops | bytes accessed | tf_op | source)
XLA Modules:
  0.0 577.9 jit_solution(4415072167542892640)
XLA Ops:
  7.2 0.0 all-gather.3.cloned.1.call-start
  7.2 0.7 all-gather.3.cloned.1.call-update
  7.9 0.1 copy.16
  8.1 0.1 reshape.182
  8.2 0.1 eq.41
  8.4 0.6 reduce-window.6
  9.0 0.2 slice_reduce_fusion.2
  9.2 0.1 fusion.15
  9.3 0.2 fusion.8
  9.5 0.1 broadcast_in_dim.35
  9.7 0.3 reshape.185
  10.0 0.2 select_reduce_fusion
  10.2 3.9 gather_fusion.1
  14.1 4.8 gather.10
  18.8 2.2 broadcast_select_fusion
  21.0 3.8 copy.20
  24.9 11.7 %all-to-all-start.1 = ((bf16[2,32,12,1536]{3,0,2,1:T(2,128)(2,1)}), bf16[2,32,12,1536]{3,0,2,1:T(2,128)(2,1)S(1)}, u32[]{:S(2)}, u32[]{:S(2)}) async-start(bf16[2,32,12,1536]{3,0,2,1:T(2,128)(2,1)} %copy.20), calls=%async_computation.1 | async-start | bytes 4718592 | tf_op jit(solution)/shard_map/all_to_all | solution.py:80
  36.6 5.7 gather_fusion
  42.2 9.8 %reshape.184 = bf16[2,32,12,4096]{3,2,1,0:T(8,128)(2,1)} reshape(bf16[768,4096]{1,0:T(8,128)(2,1)} %gather_fusion) | data formatting | bytes 12582912 | tf_op jit(solution)/shard_map/reshape | solution.py:71
  52.0 13.6 %copy.19 = bf16[2,32,12,4096]{3,0,2,1:T(2,128)(2,1)} copy(bf16[2,32,12,4096]{3,2,1,0:T(8,128)(2,1)} %reshape.184) | data formatting | bytes 12582912 | tf_op jit(solution)/shard_map/reshape | solution.py:71
  65.6 53.0 %all-to-all-done.1 = bf16[2,32,12,1536]{3,0,2,1:T(2,128)(2,1)S(1)} async-done(((bf16[2,32,12,1536]{3,0,2,1:T(2,128)(2,1)}), bf16[2,32,12,1536]{3,0,2,1:T(2,128)(2,1)S(1)}, u32[]{:S(2)}, u32[]{:S(2)}) %all-to-all-start.1) | async-done | bytes 2359328 | tf_op jit(solution)/shard_map/all_to_all | solution.py:80
  118.6 5.3 all-to-all-start
  123.9 0.2 all-reduce.3.cloned.1.call-start
  124.1 15.0 %fusion.5 = (f32[32,12,1536]{2,1,0:T(8,128)}, f32[32,12,1536]{2,1,0:T(8,128)}) fusion(bf16[2,32,12,1536]{3,0,2,1:T(2,128)(2,1)S(1)} %all-to-all-done.1), kind=kLoop, calls=%fused_computation.16 | loop fusion | flops 1179648 | bytes 7077888 | tf_op jit(solution)/shard_map/convert_element_type | solution.py:36
  139.1 3.6 reshape.187
  142.7 3.6 reshape.188
  146.3 186.3 %all-to-all-done = bf16[2,32,12,4096]{3,0,2,1:T(2,128)(2,1)} async-done(((bf16[2,32,12,4096]{3,0,2,1:T(2,128)(2,1)}), bf16[2,32,12,4096]{3,0,2,1:T(2,128)(2,1)}, u32[]{:S(2)}, u32[]{:S(2)}) %all-to-all-start) | async-done | bytes 6291488 | tf_op jit(solution)/shard_map/all_to_all | solution.py:79
  332.6 33.0 %slice_reduce_fusion.1 = (bf16[32,12,4096]{2,1,0:T(8,128)(2,1)}, bf16[32,12,4096]{2,1,0:T(8,128)(2,1)}) fusion(bf16[2,32,12,4096]{3,0,2,1:T(2,128)(2,1)} %all-to-all-done), kind=kLoop, calls=%fused_computation.3 | loop fusion | bytes 12582912 | tf_op jit(solution)/shard_map/slice | solution.py:85
  365.6 5.7 squeeze.26
  371.2 5.6 squeeze.30
  376.9 3.0 convolution_convert_fusion.3
  379.9 0.9 convolution_convert_fusion.1
  380.8 69.0 %all-gather.3.cloned.1.call-done = bf16[16,512,1536]{2,1,0:T(8,128)(2,1)} async-done(((bf16[2,512,1536]{2,1,0:T(8,128)(2,1)}), bf16[16,512,1536]{2,1,0:T(8,128)(2,1)}) %all-gather.3.cloned.1.call-update) | async-done | bytes 25165840 | tf_op jit(solution)/shard_map/all_gather | solution.py:10
  449.8 13.8 %fusion.33 = (bf16[1,8,512,1536]{3,2,0,1:T(8,128)(2,1)S(1)}, bf16[1,8,512,1536]{3,2,0,1:T(8,128)(2,1)}) fusion(bf16[2,8,512,1536]{3,2,0,1:T(8,128)(2,1)} %bitcast.66), kind=kLoop, calls=%fused_computation.71 | loop fusion | bytes 50331648 | tf_op jit(solution)/shard_map/slice | solution.py:92
  463.6 5.1 fusion.34
  468.7 1.1 multiply_convert_fusion.1
  469.9 3.0 fusion.1
  472.9 0.3 fusion.6
  473.1 9.1 %fusion.35 = f32[384,1536]{1,0:T(8,128)S(1)} fusion(bf16[384,4096]{1,0:T(8,128)(2,1)} %squeeze.30, bf16[4096,1536]{1,0:T(8,128)(2,1)} %bitcast.67), kind=kOutput, calls=%fused_computation.73 | convolution fusion | flops 4831838208 | bytes 18087936 | tf_op jit(solution)/shard_map/dot_general | solution.py:21
  482.2 1.1 multiply_convert_fusion
  483.4 3.1 fusion
  486.4 0.3 fusion.7
  486.7 0.7 pad_maximum_fusion.1
  487.4 0.8 pad_maximum_fusion
  488.3 0.0 all-reduce.3.cloned.1.call-update
  488.3 79.3 %all-reduce.3.cloned.1.call-done = (f32[2,4096,16]{1,2,0:T(8,128)}, f32[2,16,1536]{2,1,0:T(8,128)}) async-done(((f32[2,4096,16]{1,2,0:T(8,128)}, f32[2,16,1536]{2,1,0:T(8,128)}), (f32[2,4096,16]{1,2,0:T(8,128)}, f32[2,16,1536]{2,1,0:T(8,128)})) %all-reduce.3.cloned.1.call-update) | async-done | bytes 720912 | tf_op jit(solution)/shard_map/psum | solution.py:110
  567.6 1.9 copy.29
  569.4 1.6 copy.30
  (26 shorter events, 0.2 us)
Async XLA Ops:
  7.2 29.4 %copy-start = (bf16[128,4096]{1,0:T(8,128)(2,1)S(1)}, bf16[128,4096]{1,0:T(8,128)(2,1)}, u32[]{:S(2)}) copy-start(bf16[128,4096]{1,0:T(8,128)(2,1)} %param.6) | copy-start | bytes 3145732
  7.2 0.8 copy-start.9
  7.2 2.5 copy-start.6
  7.2 442.6 %all-gather.3.cloned.1.call-start = ((), (), s32[]{:S(2)}) async-start(), calls=%async_computation.2 | async-start | bytes 28311552 | tf_op jit(solution)/shard_map/all_gather | solution.py:10
  24.9 93.7 %all-to-all-start.1 = ((bf16[2,32,12,1536]{3,0,2,1:T(2,128)(2,1)}), bf16[2,32,12,1536]{3,0,2,1:T(2,128)(2,1)S(1)}, u32[]{:S(2)}, u32[]{:S(2)}) async-start(bf16[2,32,12,1536]{3,0,2,1:T(2,128)(2,1)} %copy.20), calls=%async_computation.1 | async-start | bytes 4718592 | tf_op jit(solution)/shard_map/all_to_all | solution.py:80
  118.6 214.0 %all-to-all-start = ((bf16[2,32,12,4096]{3,0,2,1:T(2,128)(2,1)}), bf16[2,32,12,4096]{3,0,2,1:T(2,128)(2,1)}, u32[]{:S(2)}, u32[]{:S(2)}) async-start(bf16[2,32,12,4096]{3,0,2,1:T(2,128)(2,1)} %copy.19), calls=%async_computation | async-start | bytes 12582912 | tf_op jit(solution)/shard_map/all_to_all | solution.py:79
  123.9 443.6 %all-reduce.3.cloned.1.call-start = ((), (), s32[]{:S(2)}) async-start(), calls=%async_computation.3 | async-start | bytes 1441792 | tf_op jit(solution)/shard_map/psum | solution.py:110
  371.2 5.6 copy-start.7
  376.9 3.0 copy-start.2
  449.8 13.8 %copy-start.3 = (bf16[384,4096]{1,0:T(8,128)(2,1)S(1)}, bf16[384,4096]{1,0:T(8,128)(2,1)}, u32[]{:S(2)}) copy-start(bf16[384,4096]{1,0:T(8,128)(2,1)} %squeeze.26) | copy-start | bytes 9437188
  463.6 5.1 copy-start.5
  463.6 5.1 copy-start.8
  473.1 9.1 %copy-start.4 = (f32[384,1536]{1,0:T(8,128)S(1)}, f32[384,1536]{1,0:T(8,128)}, u32[]{:S(2)}) copy-start(f32[384,1536]{1,0:T(8,128)} %reshape.188) | copy-start | bytes 7077892
  483.4 87.7 %copy-start.1 = (bf16[128,4096]{1,0:T(8,128)(2,1)S(1)}, bf16[128,4096]{1,0:T(8,128)(2,1)}, u32[]{:S(2)}) copy-start(bf16[128,4096]{1,0:T(8,128)(2,1)} %param.6) | copy-start | bytes 3145732
Sparse Core Ops, SparseCore 0:
  9.8 439.9 all-gather.2
  488.4 79.1 all-reduce.2
